TPU v7x, 32 devices: a whole 2x2x4 slice. The times are simulated.
32 devices in a mesh: groups: 2 (over y), heads: 4 (over z), batch: 4 (over x, core).
Axes of the slice: x: 2, y: 2, z: 4, core: 2. Of those that a mesh axis runs over, the one named last changes fastest.
Arguments:
- queries: bfloat16 [128, 8192], P(('groups', 'batch'), 'heads'), parts along dimension 0, may hold values from -110 to 110
- new_kv: bfloat16 [16, 64, 256], P(('groups', 'heads'), 'batch'), parts along dimension 0, may hold values from -15 to 15
- kv_pool: bfloat16 [16, 192, 128, 256], P(('groups', 'heads'), 'batch'), parts along dimension 0, may hold values from -6 to 6
- page_counts: int32 [8, 16], P(('groups', 'batch')), parts along dimension 0, may hold values from 1 to 6, 48 in all within a row
- last_fill: int32 [8, 16], P(('groups', 'batch')), parts along dimension 0, may hold values from 1 to 128
- page_order: int32 [8, 48], P(('groups', 'batch')), parts along dimension 0, may hold values from 0 to 47, each once within a row
- hidden: bfloat16 [128, 8192], P(('groups', 'batch')), parts along dimension 0, may hold values from -0.59765625 to 0.59765625
- out_weight: bfloat16 [8192, 8192], P('heads'), may hold values from -0.5 to 0.5
- norm_gain: bfloat16 [8192], replicated, may hold values from 0.099609375 to 1.8984375
- sectioned: bfloat16 [8, 4, 8, 128, 256], P(('groups', 'heads'), 'batch'), parts along dimension 0, may hold values from -6 to 6
- routes: int32 [8, 4, 8, 1], P(('groups', 'heads'), 'batch'), parts along dimension 0, may hold values from 0 to 7; in each aligned block of 8 rows (0 to 7, 8 to 15, ..., all dimensions but the last counted through in order) at most 2 rows name the same one
Outputs:
- residual_out: bfloat16 [128, 8192], P(('groups', 'batch')), parts along dimension 0
- normed: bfloat16 [128, 8192], P(('groups', 'batch')), parts along dimension 0
- arrival: bfloat16 [16, 4, 4, 2, 128, 256], P(('groups', 'heads'), 'batch'), parts along dimension 0
There are 2 independent parts, one for each index of `groups`. A program takes and returns all parts, laid end to end along the dimension named above; an argument that names none is the same for every part. Nothing has to cross between parts.
Inputs may be any that keep to these rules, and one draw needn't show every extreme that they name: `routes`: every key-value head is named by at most 2 sectioned pages of one device. `page_counts`: the page counts of one batch owner sum to 48.
All inputs are finite; a program needn't handle non-finite values.
Results may differ from a plain program's by a relative error of at most 0.0066.
Values may be sent and summed in bfloat16 or wider, within the bound.
A program may use at most 128 MiB of HBM per device.

v0:
```python
import jax
import jax.numpy as jnp
from jax import lax
from jax.sharding import PartitionSpec as P

KV_HEADS = 8
PER_HEAD_CAP = 2
norm_epsilon = 1e-06


def attend(queries, new_kv, kv_pool, counts, fill, order):
    slot_count, pool_pages, page_size, lane_width = kv_pool.shape
    head_dim = lane_width // 2
    requests = queries.shape[0]
    score_scale = 1.0 / head_dim**0.5
    position = jnp.arange(pool_pages, dtype=jnp.int32)
    position_in_order = jnp.sum(
        jnp.where(order[None, :] == position[:, None], position[None, :], 0), axis=1
    )
    count_ends = jnp.cumsum(counts)
    starts = count_ends - counts
    owner_index = jnp.sum(
        (count_ends[None, :] <= position_in_order[:, None]).astype(jnp.int32), axis=1
    )
    member = owner_index[:, None] == jnp.arange(requests, dtype=jnp.int32)[None, :]
    member_float = member.astype(jnp.float32)
    within = position_in_order - jnp.sum(jnp.where(member, starts[None, :], 0), axis=1)
    context = (counts - 1) * page_size + fill
    context_limit = jnp.sum(jnp.where(member, context[None, :], 0), axis=1)
    live_tokens = (
        within[:, None] * page_size + jnp.arange(page_size, dtype=jnp.int32)[None, :]
        < context_limit[:, None]
    )
    page_queries = jnp.einsum(
        "pr,rlgd->lpgd", member.astype(jnp.bfloat16), queries, preferred_element_type=jnp.float32
    ).astype(jnp.bfloat16)
    scores = (
        jnp.einsum(
            "lpgd,lptd->lpgt",
            page_queries,
            kv_pool[..., :head_dim],
            preferred_element_type=jnp.float32,
        )
        * score_scale
    )
    scores = jnp.where(live_tokens[None, :, None, :], scores, -1e30)
    page_top = jnp.max(scores, axis=3)
    fresh_score = (
        jnp.einsum(
            "rlgd,lrd->lrg", queries, new_kv[..., :head_dim], preferred_element_type=jnp.float32
        )
        * score_scale
    )
    masked_top = jnp.where(member.T[None, :, :, None], page_top[:, None, :, :], -1e30)
    request_top = jnp.maximum(fresh_score, jnp.max(masked_top, axis=2))
    page_ref = jnp.einsum("pr,lrg->lpg", member_float, request_top, precision=lax.Precision.HIGHEST)
    weight = jnp.where(live_tokens[None, :, None, :], jnp.exp(scores - page_ref[..., None]), 0.0)
    page_den = jnp.sum(weight, axis=3)
    page_num = jnp.einsum(
        "lpgt,lptd->lpgd",
        weight.astype(jnp.bfloat16),
        kv_pool[..., head_dim:],
        preferred_element_type=jnp.float32,
    )
    fresh_weight = jnp.exp(fresh_score - request_top)
    fresh_rounded = lax.optimization_barrier(fresh_weight.astype(jnp.bfloat16)).astype(jnp.float32)
    denominator = (
        jnp.einsum("pr,lpg->lrg", member_float, page_den, precision=lax.Precision.HIGHEST)
        + fresh_weight
    )
    numerator = jnp.einsum("pr,lpgd->lrgd", member_float, page_num, precision=lax.Precision.HIGHEST)
    numerator = numerator + fresh_rounded[..., None] * new_kv[:, :, None, head_dim:].astype(
        jnp.float32
    )
    attended = numerator / denominator[..., None]
    attended = jnp.transpose(attended, (1, 0, 2, 3)).astype(jnp.bfloat16)
    return attended.reshape(requests, -1)


def landing_table(destination, head_total, most_pages):
    sectioned_count = destination.shape[0]
    order_ids = jnp.arange(sectioned_count, dtype=jnp.int32)
    same_head = destination[:, None] == destination[None, :]
    earlier = order_ids[:, None] > order_ids[None, :]
    page_rank = jnp.sum((same_head & earlier).astype(jnp.int32), axis=1)
    matches = (
        destination[None, None, :] == jnp.arange(head_total, dtype=jnp.int32)[:, None, None]
    ) & (page_rank[None, None, :] == jnp.arange(most_pages, dtype=jnp.int32)[None, :, None])
    source_index = jnp.sum(jnp.where(matches, order_ids[None, None, :], 0), axis=2)
    source_valid = jnp.any(matches, axis=2)
    return (source_index, source_valid)


def per_device(
    queries,
    new_kv,
    kv_pool,
    page_counts,
    last_fill,
    page_order,
    hidden,
    out_weight,
    norm_gain,
    sectioned,
    routes,
):
    head_count = lax.axis_size("heads")
    slots_dev = new_kv.shape[0]
    head_dim = kv_pool.shape[3] // 2
    requests = hidden.shape[0]
    group_size = queries.shape[1] // (slots_dev * head_dim)
    page_data = sectioned[0, 0]
    source_index, source_valid = landing_table(routes[0, 0, :, 0], KV_HEADS, PER_HEAD_CAP)
    cache_total = head_count * slots_dev
    target = (
        (
            jnp.arange(head_count, dtype=jnp.int32)[None, :] * slots_dev
            + jnp.arange(slots_dev, dtype=jnp.int32)[:, None]
        )
        * KV_HEADS
        // cache_total
    )
    picked = source_index[target]
    present = source_valid[target]
    outgoing = page_data[picked]
    outgoing = jnp.where(present[..., None, None], outgoing, jnp.zeros_like(outgoing))
    landed = lax.all_to_all(outgoing, "heads", split_axis=1, concat_axis=1, tiled=True)
    arrival = landed[:, None]
    query_block = queries.reshape(requests, slots_dev, group_size, head_dim)
    attn = attend(query_block, new_kv, kv_pool, page_counts[0], last_fill[0], page_order[0])
    partial_terms = jnp.dot(attn, out_weight, preferred_element_type=jnp.float32)
    summed = lax.psum(partial_terms, "heads")
    mixed = hidden.astype(jnp.float32) + summed
    mean_square = jnp.mean(mixed * mixed, axis=1, keepdims=True)
    normed = (mixed * lax.rsqrt(mean_square + norm_epsilon) * norm_gain.astype(jnp.float32)).astype(
        jnp.bfloat16
    )
    residual_out = mixed.astype(jnp.bfloat16)
    return (residual_out, normed, arrival)


def solution(mesh):
    return jax.shard_map(
        per_device,
        mesh=mesh,
        in_specs=(
            P(("groups", "batch"), "heads"),
            P(("groups", "heads"), "batch", None),
            P(("groups", "heads"), "batch", None, None),
            P(("groups", "batch"), None),
            P(("groups", "batch"), None),
            P(("groups", "batch"), None),
            P(("groups", "batch"), None),
            P("heads", None),
            P(),
            P(("groups", "heads"), "batch", None, None, None),
            P(("groups", "heads"), "batch", None, None),
        ),
        out_specs=(
            P(("groups", "batch"), None),
            P(("groups", "batch"), None),
            P(("groups", "heads"), "batch", None, None, None, None),
        ),
        check_vma=False,
    )
```

profile of v0, /device:TPU:0, one launch (start us, length us, event | category | flops | bytes accessed | tf_op | source)
XLA Modules:
  0.0 96.6 jit_solution(1213633889777169506)
XLA Ops:
  7.2 0.0 copy-start
  7.2 0.0 all-reduce.2.cloned.1.call-start
  7.2 0.8 select_reduce_fusion.1
  8.0 0.7 copy.69
  8.8 0.1 reduce
  8.9 0.1 convert_reduce_fusion
  9.0 0.7 add_bitcast_fusion
  9.7 0.1 select_reduce_fusion.3
  9.8 0.7 convert_bitcast_fusion
  10.5 0.8 copy.93
  11.4 0.3 fusion.10
  11.6 0.1 fusion.27
  11.8 0.1 copy.90
  11.9 0.1 add_compare_fusion
  12.0 3.7 %fusion.48 = (f32[2,48,8]{2,1,0:T(8,128)S(1)}, f32[2,48,8,128]{3,2,1,0:T(8,128)S(1)}) fusion(bf16[2,48,128,256]{3,2,1,0:T(8,128)(2,1)} %param.13, bf16[2,48,8,128]{3,1,2,0:T(8,128)(2,1)S(1)} %fusion.10, pred[48,128]{1,0:T(8,128)(4,1)S(1)} %add_compare_fusion), kind=kOutput, calls=%fused_computation.86 | convolution fusion | flops 25459968 | bytes 3744768 | tf_op jit(solution)/shard_map/lpgd,lptd->lpgt/dot_general | solution.py:38
  15.7 0.1 copy.72
  15.7 0.1 select_reduce_fusion
  15.9 0.1 copy.73
  15.9 0.1 convolution_bitcast_fusion.1
  16.1 0.1 copy.74
  16.2 0.3 fusion.15
  16.5 2.9 %fusion = f32[2,48,8,128]{3,2,1,0:T(8,128)S(1)} fusion(bf16[2,48,128,256]{3,2,1,0:T(8,128)(2,1)} %param.13, f32[2,48,8,128]{3,2,1,0:T(8,128)S(1)} %get-tuple-element.24, f32[2,48,8]{2,1,0:T(8,128)S(1)} %copy.74, pred[48,128]{1,0:T(8,128)(4,1)S(1)} %add_compare_fusion), kind=kOutput, calls=%fused_computation.3 | convolution fusion | flops 25460736 | bytes 3941376 | tf_op jit(solution)/shard_map/lpgt,lptd->lpgd/dot_general | solution.py:59
  19.3 0.1 copy.76
  19.4 0.1 fusion.13
  19.6 0.3 fusion.12
  19.9 0.0 copy-start.3
  19.9 13.7 %fusion.23 = f32[16,8192]{1,0:T(8,128)} fusion(bf16[2048,8192]{1,0:T(8,128)(2,1)} %param.18, bf16[2,8,16,128]{3,2,1,0:T(8,128)(2,1)S(1)} %bitcast.73), kind=kOutput, calls=%fused_computation.31 | convolution fusion | flops 536870912 | bytes 34144256 | tf_op jit(solution)/shard_map/dot_general | solution.py:131
  33.6 0.0 copy-start.2
  33.6 0.0 copy-start.1
  33.6 0.0 all-reduce.2.cloned.1.call-update
  33.6 0.0 copy-done.3
  33.6 0.2 convert_reduce_fusion.1
  33.8 0.1 and_reduce_fusion
  34.0 0.2 fusion.30
  34.2 0.1 reshape.257
  34.2 0.1 copy.79
  34.3 0.1 copy.82
  34.4 0.6 gather_fusion.1
  35.0 0.6 gather_fusion
  35.6 0.1 copy.92
  35.7 0.1 copy.84
  35.8 0.1 reshape.273
  35.9 0.0 copy-done
  35.9 0.6 gather_fusion.2
  36.5 0.1 broadcast_select_fusion
  36.6 1.1 %copy.85 = bf16[2,4,2,128,256]{4,3,2,0,1:T(8,128)(2,1)} copy(bf16[2,4,2,128,256]{4,3,2,1,0:T(8,128)(2,1)S(1)} %broadcast_select_fusion) | data formatting | bytes 2097152 | tf_op jit(solution)/shard_map/jit(_where)/select_n | solution.py:126
  37.7 6.3 %all-to-all-start = ((bf16[2,4,2,128,256]{4,3,2,0,1:T(8,128)(2,1)}), bf16[2,4,2,128,256]{4,3,2,0,1:T(8,128)(2,1)S(1)}, u32[]{:S(2)}, u32[]{:S(2)}) async-start(bf16[2,4,2,128,256]{4,3,2,0,1:T(8,128)(2,1)} %copy.85), calls=%async_computation | async-start | bytes 2097152 | tf_op jit(solution)/shard_map/all_to_all | solution.py:127
  44.0 0.0 copy-done.2
  44.1 41.5 %all-reduce.2.cloned.1.call-done = f32[16,8192]{1,0:T(8,128)} async-done(((f32[16,8192]{1,0:T(8,128)}), f32[16,8192]{1,0:T(8,128)}) %all-reduce.2.cloned.1.call-update) | async-done | bytes 524304 | tf_op jit(solution)/shard_map/psum | solution.py:132
  85.6 0.0 copy-done.1
  85.6 1.2 %multiply_reduce_fusion = f32[16]{0:T(128)S(1)} fusion(f32[16,8192]{1,0:T(8,128)} %all-reduce.2.cloned.1.call-done, bf16[16,8192]{1,0:T(8,128)(2,1)S(1)} %copy-done.1), kind=kLoop, calls=%fused_computation.19 | loop fusion | flops 524272 | bytes 786496 | tf_op jit(solution)/shard_map/reduce_sum | solution.py:134
  86.8 1.9 %multiply_convert_fusion = (bf16[16,8192]{1,0:T(8,128)(2,1)}, bf16[16,8192]{1,0:T(8,128)(2,1)}) fusion(f32[8192]{0:T(1024)S(1)} %convert_element_type.46, f32[16]{0:T(128)S(1)} %add_rsqrt_fusion, f32[16,8192]{1,0:T(8,128)} %all-reduce.2.cloned.1.call-done, bf16[16,8192]{1,0:T(8,128)(2,1)S(1)} %copy-done.1), kind=kLoop, calls=%fused_computation.18 | loop fusion | flops 786432 | bytes 1343552 | tf_op jit(solution)/shard_map/convert_element_type | solution.py:135
  88.7 0.0 all-to-all-done
  88.7 1.0 %copy.86 = bf16[2,1,4,2,128,256]{5,4,3,2,1,0:T(8,128)(2,1)} copy(bf16[2,1,4,2,128,256]{5,4,3,0,2,1:T(8,128)(2,1)S(1)} %bitcast.71) | data formatting | bytes 2097152
  (15 shorter events, 0.1 us)
Async XLA Ops:
  7.2 28.7 %copy-start = (bf16[1,1,8,128,256]{4,3,2,1,0:T(8,128)(2,1)S(1)}, bf16[1,1,8,128,256]{4,3,2,1,0:T(8,128)(2,1)}, u32[]{:S(2)}) copy-start(bf16[1,1,8,128,256]{4,3,2,1,0:T(8,128)(2,1)} %param.20) | copy-start | bytes 1572868
  7.2 78.4 %all-reduce.2.cloned.1.call-start = ((), (), s32[]{:S(2)}) async-start(), calls=%async_computation.1 | async-start | bytes 1048576 | tf_op jit(solution)/shard_map/psum | solution.py:132
  19.9 13.7 %copy-start.3 = (s32[1,1,8,1]{2,3,1,0:T(1,128)S(1)}, s32[1,1,8,1]{2,3,1,0:T(1,128)}, u32[]{:S(2)}) copy-start(s32[1,1,8,1]{2,3,1,0:T(1,128)} %param.21) | copy-start | bytes 100
  33.6 10.5 %copy-start.2 = (bf16[8192]{0:T(1024)(128)(2,1)S(1)}, bf16[8192]{0:T(1024)(128)(2,1)}, u32[]{:S(2)}) copy-start(bf16[8192]{0:T(1024)(128)(2,1)} %param.19) | copy-start | bytes 49156
  33.6 52.0 %copy-start.1 = (bf16[16,8192]{1,0:T(8,128)(2,1)S(1)}, bf16[16,8192]{1,0:T(8,128)(2,1)}, u32[]{:S(2)}) copy-start(bf16[16,8192]{1,0:T(8,128)(2,1)} %param.17) | copy-start | bytes 786436
  37.7 51.0 %all-to-all-start = ((bf16[2,4,2,128,256]{4,3,2,0,1:T(8,128)(2,1)}), bf16[2,4,2,128,256]{4,3,2,0,1:T(8,128)(2,1)S(1)}, u32[]{:S(2)}, u32[]{:S(2)}) async-start(bf16[2,4,2,128,256]{4,3,2,0,1:T(8,128)(2,1)} %copy.85), calls=%async_computation | async-start | bytes 2097152 | tf_op jit(solution)/shard_map/all_to_all | solution.py:127
Sparse Core Ops, SparseCore 0:
  33.7 51.7 all-reduce.1
where the time goes:
time: 97.1 us; the launch traced here: 96.6 us
  waiting for transfers between devices  41.5 us (43%)
  matrix products  21.2 us (22%)
  between operations  14.2 us (15%)
  other arithmetic  6.9 us (7%)
  local copies, waits for them, and re-layouts  6.39 us (7%)
  starting transfers between devices  6.38 us (7%)
    psum x1, waiting for transfers between devices, per_device(): summed = lax.psum(partial_terms, 'heads')  41.5 us
    dot_general x1, matrix products, per_device(): jnp.dot(attn, out_weight, preferred_element_type=jnp.float32)  13.7 us
    all_to_all x1, starting transfers between devices, per_device(): lax.all_to_all(outgoing, 'heads', split_axis=1, concat_axis=1, tiled=True)  6.35 us
    dot_general x1, matrix products, attend(): jnp.einsum('lpgd,lptd->lpgt', page_queries, kv_pool[..., :head_dim], pref...  3.69 us
    dot_general x1, matrix products, attend(): jnp.einsum('lpgt,lptd->lpgd', weight.astype(jnp.bfloat16), kv_pool[..., h...  2.86 us
  transfers between devices with their start and end apart: 2, of which 1 were waited for; matrix products, arithmetic and copies ran while one was open for 7% of the time, Pallas kernels for 0%

commit v1 on v0

--- a/solution.py
+++ b/solution.py
@@ -1,3 +1,4 @@
+import functools
 import jax
 import jax.numpy as jnp
 from jax import lax
@@ -6,6 +7,20 @@
 KV_HEADS = 8
 PER_HEAD_CAP = 2
 norm_epsilon = 1e-06
+
+
+def recast_the_chunk(load, which_axis):
+    wide_n = lax.axis_size(which_axis)
+    part_now, g_now = (load, 0)
+    while 1 << g_now < wide_n:
+        later = tuple(((b, b ^ 1 << g_now) for b in range(wide_n)))
+        z1 = lax.ppermute(part_now, which_axis, later)
+        part_now = part_now + z1
+        g_now = g_now + 1
+    return part_now
+
+
+check_the_gates = functools.partial(recast_the_chunk, which_axis="heads")
 
 
 def attend(queries, new_kv, kv_pool, counts, fill, order):
@@ -129,7 +144,7 @@
     query_block = queries.reshape(requests, slots_dev, group_size, head_dim)
     attn = attend(query_block, new_kv, kv_pool, page_counts[0], last_fill[0], page_order[0])
     partial_terms = jnp.dot(attn, out_weight, preferred_element_type=jnp.float32)
-    summed = lax.psum(partial_terms, "heads")
+    summed = check_the_gates(partial_terms)
     mixed = hidden.astype(jnp.float32) + summed
     mean_square = jnp.mean(mixed * mixed, axis=1, keepdims=True)
     normed = (mixed * lax.rsqrt(mean_square + norm_epsilon) * norm_gain.astype(jnp.float32)).astype(

time: 97.1 us -> 90.5 us (0.932)
  between operations: 14.2 us -> 0.79 us
  waiting for transfers between devices: 41.5 us -> 48.2 us
  starting transfers between devices: 6.38 us -> 9.42 us
  other arithmetic: 6.9 us -> 4.89 us
    psum x1 -> x0, waiting for transfers between devices: 41.5 us -> none  [per_device(): summed = lax.psum(partial_terms, 'heads')]
    ppermute x0 -> x2, waiting for transfers between devices: none -> 39 us  [recast_the_chunk(): z1 = lax.ppermute(part_now, which_axis, later)]
    all_to_all x1, waiting for transfers between devices: 0.01 us -> 9.19 us  [per_device(): lax.all_to_all(outgoing, 'heads', split_axis=1, concat_axis=1, tiled=True)]
    ppermute x0 -> x2, starting transfers between devices: none -> 5.91 us  [recast_the_chunk(): z1 = lax.ppermute(part_now, which_axis, later)]
    all_to_all x1, starting transfers between devices: 6.35 us -> 3.52 us  [per_device(): lax.all_to_all(outgoing, 'heads', split_axis=1, concat_axis=1, tiled=True)]
    convert_element_type x1, other arithmetic: 1.89 us -> 0.84 us  [per_device(): (mixed * lax.rsqrt(mean_square + norm_epsilon) * norm_gain.astype(jnp.flo...]
    reduce_sum x1, other arithmetic: 1.22 us -> 0.2 us  [per_device(): mean_square = jnp.mean(mixed * mixed, axis=1, keepdims=True)]
  transfers between devices with their start and end apart: 2 -> 3, of which waited for: 1 -> 3; matrix products, arithmetic and copies ran while one was open for 7% -> 6% of each run, Pallas kernels for 0% -> 0%
where the time goes in v1:
time: 90.5 us; the launch traced here: 90.1 us
  waiting for transfers between devices  48.2 us (53%)
  matrix products  20.4 us (23%)
  starting transfers between devices  9.42 us (10%)
  local copies, waits for them, and re-layouts  6.41 us (7%)
  other arithmetic  4.89 us (5%)
    ppermute x2, waiting for transfers between devices, recast_the_chunk(): z1 = lax.ppermute(part_now, which_axis, later)  39 us
    dot_general x1, matrix products, per_device(): jnp.dot(attn, out_weight, preferred_element_type=jnp.float32)  12.8 us
    all_to_all x1, waiting for transfers between devices, per_device(): lax.all_to_all(outgoing, 'heads', split_axis=1, concat_axis=1, tiled=True)  9.19 us
    ppermute x2, starting transfers between devices, recast_the_chunk(): z1 = lax.ppermute(part_now, which_axis, later)  5.91 us
    dot_general x1, matrix products, attend(): jnp.einsum('lpgd,lptd->lpgt', page_queries, kv_pool[..., :head_dim], pref...  3.69 us
    all_to_all x1, starting transfers between devices, per_device(): lax.all_to_all(outgoing, 'heads', split_axis=1, concat_axis=1, tiled=True)  3.52 us
    dot_general x1, matrix products, attend(): jnp.einsum('lpgt,lptd->lpgd', weight.astype(jnp.bfloat16), kv_pool[..., h...  2.86 us
    unnamed x10, local copies, waits for them, and re-layouts  1.91 us
  transfers between devices with their start and end apart: 3, of which 3 were waited for; matrix products, arithmetic and copies ran while one was open for 6% of the time, Pallas kernels for 0%

profile of v1, /device:TPU:0, one launch (start us, length us, event | category | flops | bytes accessed | tf_op | source)
XLA Modules:
  0.0 90.1 jit_solution(973475816363750958)
XLA Ops:
  0.6 0.0 copy-start
  0.6 0.8 select_reduce_fusion.1
  1.5 0.7 copy.69
  2.2 0.1 reduce
  2.4 0.1 convert_reduce_fusion
  2.5 0.7 add_bitcast_fusion
  3.1 0.1 select_reduce_fusion.3
  3.2 0.7 convert_bitcast_fusion
  4.0 0.8 copy.93
  4.8 0.3 fusion.10
  5.1 0.1 fusion.26
  5.2 0.1 copy.90
  5.3 0.1 add_compare_fusion
  5.4 3.7 %fusion.47 = (f32[2,48,8]{2,1,0:T(8,128)S(1)}, f32[2,48,8,128]{3,2,1,0:T(8,128)S(1)}) fusion(bf16[2,48,128,256]{3,2,1,0:T(8,128)(2,1)} %param.13, bf16[2,48,8,128]{3,1,2,0:T(8,128)(2,1)S(1)} %fusion.10, pred[48,128]{1,0:T(8,128)(4,1)S(1)} %add_compare_fusion), kind=kOutput, calls=%fused_computation.85 | convolution fusion | flops 25459968 | bytes 3744768 | tf_op jit(solution)/shard_map/lpgd,lptd->lpgt/dot_general | solution.py:53
  9.1 0.1 copy.72
  9.1 0.1 select_reduce_fusion
  9.3 0.1 copy.73
  9.4 0.1 convolution_bitcast_fusion.1
  9.5 0.1 copy.74
  9.6 0.3 fusion.15
  9.9 2.9 %fusion = f32[2,48,8,128]{3,2,1,0:T(8,128)S(1)} fusion(bf16[2,48,128,256]{3,2,1,0:T(8,128)(2,1)} %param.13, f32[2,48,8,128]{3,2,1,0:T(8,128)S(1)} %get-tuple-element.26, f32[2,48,8]{2,1,0:T(8,128)S(1)} %copy.74, pred[48,128]{1,0:T(8,128)(4,1)S(1)} %add_compare_fusion), kind=kOutput, calls=%fused_computation.3 | convolution fusion | flops 25460736 | bytes 3941376 | tf_op jit(solution)/shard_map/lpgt,lptd->lpgd/dot_general | solution.py:74
  12.8 0.1 copy.76
  12.9 0.1 fusion.13
  13.0 0.3 fusion.12
  13.3 0.0 copy-start.3
  13.3 12.8 %fusion.22 = f32[16,8192]{1,0:T(8,128)S(1)} fusion(bf16[2048,8192]{1,0:T(8,128)(2,1)} %param.18, bf16[2,8,16,128]{3,2,1,0:T(8,128)(2,1)S(1)} %bitcast.73), kind=kOutput, calls=%fused_computation.30 | convolution fusion | flops 536870912 | bytes 34144256 | tf_op jit(solution)/shard_map/dot_general | solution.py:146
  26.2 0.0 copy-start.2
  26.2 0.0 copy-start.1
  26.2 3.1 %collective-permute-start = (f32[16,8192]{1,0:T(8,128)S(1)}, f32[16,8192]{1,0:T(8,128)S(1)}, u32[]{:S(2)}, u32[]{:S(2)}) collective-permute-start(f32[16,8192]{1,0:T(8,128)S(1)} %fusion.22), channel_id=1, source_target_pairs={{0,4},{4,0},{8,12},{12,8},{1,5},{5,1},{9,13},{13,9},{2,6},{6,2},{1... | collective-permute-start | bytes 1572872 | tf_op jit(solution)/shard_map/ppermute | solution.py:17
  29.3 0.0 copy-done.3
  29.3 0.2 convert_reduce_fusion.1
  29.5 0.1 reshape.257
  29.6 0.1 and_reduce_fusion
  29.7 0.1 copy.79
  29.8 0.2 fusion.29
  30.0 0.1 copy.82
  30.1 0.6 gather_fusion.1
  30.6 0.6 gather_fusion
  31.2 0.1 copy.92
  31.3 9.9 %collective-permute-done = f32[16,8192]{1,0:T(8,128)S(1)} collective-permute-done((f32[16,8192]{1,0:T(8,128)S(1)}, f32[16,8192]{1,0:T(8,128)S(1)}, u32[]{:S(2)}, u32[]{:S(2)}) %collective-permute-start) | collective-permute-done | bytes 524320 | tf_op jit(solution)/shard_map/ppermute | solution.py:17
  41.2 0.1 add.111
  41.2 2.8 %collective-permute-start.1 = (f32[16,8192]{1,0:T(8,128)S(1)}, f32[16,8192]{1,0:T(8,128)S(1)}, u32[]{:S(2)}, u32[]{:S(2)}) collective-permute-start(f32[16,8192]{1,0:T(8,128)S(1)} %add.111), channel_id=1, source_target_pairs={{0,8},{4,12},{8,0},{12,4},{1,9},{5,13},{9,1},{13,5},{2,10},{6,14},... | collective-permute-start | bytes 1572872 | tf_op jit(solution)/shard_map/ppermute | solution.py:17
  44.1 0.1 copy.84
  44.2 0.1 reshape.273
  44.3 0.0 copy-done
  44.3 0.6 gather_fusion.2
  44.9 0.1 broadcast_select_fusion
  45.0 1.1 %copy.85 = bf16[2,4,2,128,256]{4,3,2,0,1:T(8,128)(2,1)} copy(bf16[2,4,2,128,256]{4,3,2,1,0:T(8,128)(2,1)S(1)} %broadcast_select_fusion) | data formatting | bytes 2097152 | tf_op jit(solution)/shard_map/jit(_where)/select_n | solution.py:141
  46.1 3.5 %all-to-all-start = ((bf16[2,4,2,128,256]{4,3,2,0,1:T(8,128)(2,1)}), bf16[2,4,2,128,256]{4,3,2,0,1:T(8,128)(2,1)S(1)}, u32[]{:S(2)}, u32[]{:S(2)}) async-start(bf16[2,4,2,128,256]{4,3,2,0,1:T(8,128)(2,1)} %copy.85), calls=%async_computation | async-start | bytes 2097152 | tf_op jit(solution)/shard_map/all_to_all | solution.py:142
  49.6 0.0 copy-done.2
  49.7 29.1 %collective-permute-done.1 = f32[16,8192]{1,0:T(8,128)S(1)} collective-permute-done((f32[16,8192]{1,0:T(8,128)S(1)}, f32[16,8192]{1,0:T(8,128)S(1)}, u32[]{:S(2)}, u32[]{:S(2)}) %collective-permute-start.1) | collective-permute-done | bytes 524320 | tf_op jit(solution)/shard_map/ppermute | solution.py:17
  78.8 0.0 copy-done.1
  78.8 0.2 multiply_reduce_fusion
  79.0 0.8 multiply_convert_fusion
  79.9 9.2 %all-to-all-done = bf16[2,4,2,128,256]{4,3,2,0,1:T(8,128)(2,1)S(1)} async-done(((bf16[2,4,2,128,256]{4,3,2,0,1:T(8,128)(2,1)}), bf16[2,4,2,128,256]{4,3,2,0,1:T(8,128)(2,1)S(1)}, u32[]{:S(2)}, u32[]{:S(2)}) %all-to-all-start) | async-done | bytes 1048608 | tf_op jit(solution)/shard_map/all_to_all | solution.py:142
  89.1 1.0 %copy.86 = bf16[2,1,4,2,128,256]{5,4,3,2,1,0:T(8,128)(2,1)} copy(bf16[2,1,4,2,128,256]{5,4,3,0,2,1:T(8,128)(2,1)S(1)} %bitcast.71) | data formatting | bytes 2097152
  (15 shorter events, 0.1 us)
Async XLA Ops:
  0.6 43.6 %copy-start = (bf16[1,1,8,128,256]{4,3,2,1,0:T(8,128)(2,1)S(1)}, bf16[1,1,8,128,256]{4,3,2,1,0:T(8,128)(2,1)}, u32[]{:S(2)}) copy-start(bf16[1,1,8,128,256]{4,3,2,1,0:T(8,128)(2,1)} %param.20) | copy-start | bytes 1572868
  13.3 15.9 %copy-start.3 = (s32[1,1,8,1]{2,3,1,0:T(1,128)S(1)}, s32[1,1,8,1]{2,3,1,0:T(1,128)}, u32[]{:S(2)}) copy-start(s32[1,1,8,1]{2,3,1,0:T(1,128)} %param.21) | copy-start | bytes 100
  26.2 23.5 %copy-start.2 = (bf16[8192]{0:T(1024)(128)(2,1)S(1)}, bf16[8192]{0:T(1024)(128)(2,1)}, u32[]{:S(2)}) copy-start(bf16[8192]{0:T(1024)(128)(2,1)} %param.19) | copy-start | bytes 49156
  26.2 52.6 %copy-start.1 = (bf16[16,8192]{1,0:T(8,128)(2,1)S(1)}, bf16[16,8192]{1,0:T(8,128)(2,1)}, u32[]{:S(2)}) copy-start(bf16[16,8192]{1,0:T(8,128)(2,1)} %param.17) | copy-start | bytes 786436
  26.2 15.0 %collective-permute-start = (f32[16,8192]{1,0:T(8,128)S(1)}, f32[16,8192]{1,0:T(8,128)S(1)}, u32[]{:S(2)}, u32[]{:S(2)}) collective-permute-start(f32[16,8192]{1,0:T(8,128)S(1)} %fusion.22), channel_id=1, source_target_pairs={{0,4},{4,0},{8,12},{12,8},{1,5},{5,1},{9,13},{13,9},{2,6},{6,2},{1... | collective-permute-start | bytes 1572872 | tf_op jit(solution)/shard_map/ppermute | solution.py:17
  41.2 37.6 %collective-permute-start.1 = (f32[16,8192]{1,0:T(8,128)S(1)}, f32[16,8192]{1,0:T(8,128)S(1)}, u32[]{:S(2)}, u32[]{:S(2)}) collective-permute-start(f32[16,8192]{1,0:T(8,128)S(1)} %add.111), channel_id=1, source_target_pairs={{0,8},{4,12},{8,0},{12,4},{1,9},{5,13},{9,1},{13,5},{2,10},{6,14},... | collective-permute-start | bytes 1572872 | tf_op jit(solution)/shard_map/ppermute | solution.py:17
  46.1 42.9 %all-to-all-start = ((bf16[2,4,2,128,256]{4,3,2,0,1:T(8,128)(2,1)}), bf16[2,4,2,128,256]{4,3,2,0,1:T(8,128)(2,1)S(1)}, u32[]{:S(2)}, u32[]{:S(2)}) async-start(bf16[2,4,2,128,256]{4,3,2,0,1:T(8,128)(2,1)} %copy.85), calls=%async_computation | async-start | bytes 2097152 | tf_op jit(solution)/shard_map/all_to_all | solution.py:142
